TPU v7x, 8 devices: a whole 2x2x1 slice. The times are simulated.
8 devices in a mesh: dp: 2 (over z, y), sp: 4 (over x, core).
Axes of the slice: x: 2, y: 2, z: 1, core: 2. Of those that a mesh axis runs over, the one named last changes fastest.
Arguments:
- x_in: bfloat16 [4, 3072, 2048], P('dp', 'sp'), parts along dimension 0
- d_out: bfloat16 [4, 3072, 2048], P('dp', 'sp'), parts along dimension 0
- gain: float32 [2048], replicated
- w_q: bfloat16 [2048, 32, 64], replicated
- w_k: bfloat16 [2048, 8, 64], replicated
- w_v: bfloat16 [2048, 8, 64], replicated
- w_o: bfloat16 [32, 64, 2048], replicated
Outputs:
- output 1: bfloat16 [4, 3072, 2048], P('dp', 'sp'), parts along dimension 0
- output 2: bfloat16 [4, 3072, 2048], P('dp', 'sp'), parts along dimension 0
- output 3: float32 [4096, 32, 64], P('dp'), parts along dimension 0
- output 4: float32 [4096, 8, 64], P('dp'), parts along dimension 0
- output 5: float32 [4096, 8, 64], P('dp'), parts along dimension 0
- output 6: float32 [64, 64, 2048], P('dp'), parts along dimension 0
- output 7: float32 [4096], P('dp'), parts along dimension 0
There are 2 independent parts. A program takes and returns all parts, laid end to end along the dimension named above; an argument that names none is the same for every part.
All inputs are finite; a program needn't handle non-finite values.
Results may differ from a plain program's by a relative error of at most 0.0124877.
Values are sent between devices in bfloat16 or wider.
A program may use at most 1 GiB of HBM per device.

v0:
```python
import math
import jax
import jax.numpy as jnp
from jax import lax
from jax.sharding import PartitionSpec as P

ROPE_BASE = 1000000.0
NORM_EPS = 1e-5


def rope_tables(positions, head_dim):
    half = head_dim // 2
    inv_freq = ROPE_BASE ** (-2.0 * jnp.arange(half, dtype=jnp.float32) / head_dim)
    angle = positions[:, None] * inv_freq[None, :]
    return jnp.cos(angle), jnp.sin(angle)


def rotate(t_val, cos_t, sin_t):
    half = t_val.shape[-1] // 2
    first = t_val[..., :half]
    second = t_val[..., half:]
    cos_b = cos_t[:, None, :]
    sin_b = sin_t[:, None, :]
    return jnp.concatenate([first * cos_b - second * sin_b, second * cos_b + first * sin_b], axis=-1)


def rotate_back(grad_val, cos_t, sin_t):
    half = grad_val.shape[-1] // 2
    first = grad_val[..., :half]
    second = grad_val[..., half:]
    cos_b = cos_t[:, None, :]
    sin_b = sin_t[:, None, :]
    return jnp.concatenate([first * cos_b + second * sin_b, second * cos_b - first * sin_b], axis=-1)


def norm_forward(x_local, gain):
    x_f32 = x_local.astype(jnp.float32)
    inv_rms = lax.rsqrt(jnp.mean(x_f32 * x_f32, axis=-1, keepdims=True) + NORM_EPS)
    x_hat = x_f32 * inv_rms
    return x_hat, inv_rms, (x_hat * gain).astype(jnp.bfloat16)


def norm_backward(d_normed, x_hat, inv_rms, gain):
    d_hat = d_normed * gain
    return inv_rms * (d_hat - x_hat * jnp.mean(d_hat * x_hat, axis=-1, keepdims=True))


def project(normed, w_q, w_k, w_v, cos_t, sin_t):
    q_lin = jnp.einsum('bsd,dhe->bshe', normed, w_q, preferred_element_type=jnp.float32)
    k_lin = jnp.einsum('bsd,dhe->bshe', normed, w_k, preferred_element_type=jnp.float32)
    v_lin = jnp.einsum('bsd,dhe->bshe', normed, w_v, preferred_element_type=jnp.float32)
    return rotate(q_lin, cos_t, sin_t).astype(jnp.bfloat16), rotate(k_lin, cos_t, sin_t).astype(jnp.bfloat16), v_lin.astype(jnp.bfloat16)


def project_back(dq_lin, dk_lin, dv_val, w_q, w_k, w_v):
    d_q = jnp.einsum('bshe,dhe->bsd', dq_lin, w_q, preferred_element_type=jnp.float32)
    d_k = jnp.einsum('bshe,dhe->bsd', dk_lin, w_k, preferred_element_type=jnp.float32)
    d_v = jnp.einsum('bshe,dhe->bsd', dv_val, w_v, preferred_element_type=jnp.float32)
    return (d_q + d_k + d_v).astype(jnp.bfloat16)


def block_length(seq_q, num_q):
    return math.gcd(seq_q, max(64, 8192 // num_q))


def attention_forward(q_heads, k_heads, v_heads, q_offset):
    batch, seq_q, num_q, head_dim = q_heads.shape
    seq_k, num_kv = k_heads.shape[1], k_heads.shape[2]
    group = num_q // num_kv
    block_len = block_length(seq_q, num_q)
    scale = head_dim ** -0.5
    q_grouped = q_heads.reshape(batch, seq_q, num_kv, group, head_dim)
    key_pos = jnp.arange(seq_k)

    def one_block(block_idx):
        start = block_idx * block_len
        q_rows = lax.dynamic_slice_in_dim(q_grouped, start, block_len, axis=1)
        scores = jnp.einsum('bqkgd,btkd->bkgqt', q_rows, k_heads, preferred_element_type=jnp.float32) * scale
        q_pos = q_offset + start + jnp.arange(block_len)
        scores = jnp.where(key_pos[None, :] <= q_pos[:, None], scores, -1e30)
        row_max = jnp.max(scores, axis=-1, keepdims=True)
        exp_scores = jnp.exp(scores - row_max)
        row_sum = jnp.sum(exp_scores, axis=-1, keepdims=True)
        attn_weights = (exp_scores / row_sum).astype(jnp.bfloat16)
        out_rows = jnp.einsum('bkgqt,btkd->bqkgd', attn_weights, v_heads, preferred_element_type=jnp.float32)
        return out_rows.astype(jnp.bfloat16), row_max + jnp.log(row_sum)

    out_blocks, log_sum = lax.map(one_block, jnp.arange(seq_q // block_len))
    return jnp.moveaxis(out_blocks, 0, 1).reshape(batch, seq_q, num_q, head_dim), log_sum


def attention_backward(q_heads, k_heads, v_heads, d_heads, log_sum, q_offset):
    batch, seq_q, num_q, head_dim = q_heads.shape
    seq_k, num_kv = k_heads.shape[1], k_heads.shape[2]
    group = num_q // num_kv
    block_len = block_length(seq_q, num_q)
    num_blocks = seq_q // block_len
    scale = head_dim ** -0.5
    q_grouped = q_heads.reshape(batch, seq_q, num_kv, group, head_dim)
    d_grouped = d_heads.reshape(batch, seq_q, num_kv, group, head_dim)
    key_pos = jnp.arange(seq_k)

    def one_block(carry, inputs):
        dk_acc, dv_acc = carry
        block_idx, lse_rows = inputs
        start = block_idx * block_len
        q_rows = lax.dynamic_slice_in_dim(q_grouped, start, block_len, axis=1)
        d_rows = lax.dynamic_slice_in_dim(d_grouped, start, block_len, axis=1)
        scores = jnp.einsum('bqkgd,btkd->bkgqt', q_rows, k_heads, preferred_element_type=jnp.float32) * scale
        q_pos = q_offset + start + jnp.arange(block_len)
        scores = jnp.where(key_pos[None, :] <= q_pos[:, None], scores, -1e30)
        attn_weights = jnp.exp(scores - lse_rows)
        d_weights = jnp.einsum('bqkgd,btkd->bkgqt', d_rows, v_heads, preferred_element_type=jnp.float32).astype(jnp.bfloat16)
        delta = jnp.sum(attn_weights * d_weights, axis=-1, keepdims=True)
        d_scores = (attn_weights * (d_weights - delta) * scale).astype(jnp.bfloat16)
        dq_rows = jnp.einsum('bkgqt,btkd->bqkgd', d_scores, k_heads, preferred_element_type=jnp.float32).astype(jnp.bfloat16)
        dk_acc = dk_acc + jnp.einsum('bkgqt,bqkgd->btkd', d_scores, q_rows, preferred_element_type=jnp.float32)
        dv_acc = dv_acc + jnp.einsum('bkgqt,bqkgd->btkd', attn_weights.astype(jnp.bfloat16), d_rows, preferred_element_type=jnp.float32)
        return (dk_acc, dv_acc), dq_rows

    zeros = jnp.zeros(k_heads.shape, jnp.float32)
    (dk_acc, dv_acc), dq_blocks = lax.scan(one_block, (zeros, zeros), (jnp.arange(num_blocks), log_sum))
    return jnp.moveaxis(dq_blocks, 0, 1).reshape(batch, seq_q, num_q, head_dim), dk_acc, dv_acc


def solution(mesh):
    seq_par = mesh.shape['sp']

    def local_step(x_local, dy_local, gain, w_q, w_k, w_v, w_o):
        batch, seq_loc, d_model = x_local.shape
        num_kv, head_dim = w_k.shape[1], w_k.shape[2]
        spread = max(num_kv, seq_par) // num_kv
        offset = lax.axis_index('sp') * seq_loc
        cos_t, sin_t = rope_tables((offset + jnp.arange(seq_loc)).astype(jnp.float32), head_dim)
        x_hat, inv_rms, normed = norm_forward(x_local, gain)
        q_rot, k_rot, v_val = project(normed, w_q, w_k, w_v, cos_t, sin_t)
        k_send = k_rot
        v_send = v_val
        if spread > 1:
            k_send = jnp.repeat(k_rot, spread, axis=2)
            v_send = jnp.repeat(v_val, spread, axis=2)
        q_heads = lax.all_to_all(q_rot, 'sp', 2, 1, tiled=True)
        k_heads = lax.all_to_all(k_send, 'sp', 2, 1, tiled=True)
        v_heads = lax.all_to_all(v_send, 'sp', 2, 1, tiled=True)
        o_heads, log_sum = attention_forward(q_heads, k_heads, v_heads, 0)
        o_local = lax.all_to_all(o_heads, 'sp', 1, 2, tiled=True)
        y_proj = jnp.einsum('bshe,hed->bsd', o_local, w_o, preferred_element_type=jnp.float32)
        y_out = (x_local.astype(jnp.float32) + y_proj).astype(jnp.bfloat16)
        d_o = jnp.einsum('bsd,hed->bshe', dy_local, w_o, preferred_element_type=jnp.float32).astype(jnp.bfloat16)
        d_wo = jnp.einsum('bshe,bsd->hed', o_local, dy_local, preferred_element_type=jnp.float32)
        d_o_heads = lax.all_to_all(d_o, 'sp', 2, 1, tiled=True)
        dq_heads, dk_heads, dv_heads = attention_backward(q_heads, k_heads, v_heads, d_o_heads, log_sum, 0)
        dq_local = lax.all_to_all(dq_heads, 'sp', 1, 2, tiled=True)
        dk_local = lax.all_to_all(dk_heads.astype(jnp.bfloat16), 'sp', 1, 2, tiled=True)
        dv_local = lax.all_to_all(dv_heads.astype(jnp.bfloat16), 'sp', 1, 2, tiled=True)
        if spread > 1:
            dk_local = dk_local.reshape(batch, seq_loc, num_kv, spread, head_dim).sum(axis=3, dtype=jnp.float32).astype(jnp.bfloat16)
            dv_local = dv_local.reshape(batch, seq_loc, num_kv, spread, head_dim).sum(axis=3, dtype=jnp.float32).astype(jnp.bfloat16)
        dq_lin = rotate_back(dq_local, cos_t, sin_t).astype(jnp.bfloat16)
        dk_lin = rotate_back(dk_local, cos_t, sin_t).astype(jnp.bfloat16)
        d_normed = project_back(dq_lin, dk_lin, dv_local, w_q, w_k, w_v)
        d_wq = jnp.einsum('bsd,bshe->dhe', normed, dq_lin, preferred_element_type=jnp.float32)
        d_wk = jnp.einsum('bsd,bshe->dhe', normed, dk_lin, preferred_element_type=jnp.float32)
        d_wv = jnp.einsum('bsd,bshe->dhe', normed, dv_local, preferred_element_type=jnp.float32)
        d_x_norm = norm_backward(d_normed, x_hat, inv_rms, gain)
        d_gain = jnp.sum(d_normed * x_hat, axis=(0, 1))
        d_x = (dy_local.astype(jnp.float32) + d_x_norm).astype(jnp.bfloat16)
        d_wq, d_wk, d_wv, d_wo, d_gain = lax.psum((d_wq, d_wk, d_wv, d_wo, d_gain), 'sp')
        return y_out, d_x, d_wq, d_wk, d_wv, d_wo, d_gain

    specs_in = (P('dp', 'sp', None), P('dp', 'sp', None), P(None), P(None, None, None), P(None, None, None), P(None, None, None), P(None, None, None))
    specs_out = (P('dp', 'sp', None), P('dp', 'sp', None), P('dp', None, None), P('dp', None, None), P('dp', None, None), P('dp', None, None), P('dp'))
    return jax.shard_map(local_step, mesh=mesh, in_specs=specs_in, out_specs=specs_out, check_vma=False)
```

profile of v0, /device:TPU:0, one launch (start us, length us, event | category | flops | bytes accessed | tf_op | source)
XLA Modules:
  0.0 3533.9 jit_solution(10490733205871809552)
XLA Ops:
  48.4 17.3 fusion.88
  74.1 17.7 fusion.66
  101.2 43.3 %all-to-all-done.4 = bf16[2,768,32,64]{1,3,0,2:T(8,128)(2,1)} async-done(((bf16[2,768,32,64]{1,3,0,2:T(8,128)(2,1)}), bf16[2,768,32,64]{1,3,0,2:T(8,128)(2,1)}, u32[]{:S(2)}, u32[]{:S(2)}) %all-to-all-start.4) | async-done | bytes 6291488 | tf_op jit(solution)/shard_map/all_to_all | solution.py:151
  176.5 11.9 reshape.145
  188.3 31.9 all-to-all-done
  231.1 11.7 reshape.143
  246.8 625.7 %while.28 = (s32[]{:T(128)}, bf16[3,2,1024,2,4,64]{2,5,4,3,1,0:T(8,128)(2,1)}, f32[3,2,2,4,1024,1]{4,3,2,1,5,0:T(4,128)}, s32[3]{0:T(128)}, bf16[2,3072,2,4,64]{...) while((s32[]{:T(128)}, ...), condition=%wide.region_4.5_spmd.clone, body=%wide.region_1.4_spmd.clone.sunk | while | flops 13493060608 | bytes 624435328 | solution.py:88
  253.1 68.8 %bitcast_reduce_fusion.2 = (f32[2,2,4,1024]{3,2,1,0:T(4,128)S(1)}, f32[2,2,1024,4,3072]{4,2,3,1,0:T(8,128)}) fusion(pred[1024,3072]{1,0:T(8,128)(4,1)} %iota_compare_fusion.4, bf16[2,3072,2,64]{1,3,2,0:T(8,128)(2,1)} %get-tuple-element.353, bf16[2,3072,2,4,64]{1,4,3,2,0:T(8,128)(2,1)} %get-tuple-element.352, s32[]{:T(128)S(6)} %select_n.50), kind=kOutput, calls=%fused_computation.3.clone.2 | convolution fusion | flops 6593429504 | bytes 208207872 | tf_op jit(solution)/shard_map/while/body/eval_jaxpr/bqkgd,btkd->bkgqt/dot_general | solution.py:78
  321.9 63.0 %fusion.152 = f32[2,2,4,1024]{3,2,1,0:T(4,128)S(1)} fusion(f32[2,2,1024,4,3072]{4,2,3,1,0:T(8,128)} %get-tuple-element.314, f32[2,2,4,1024]{3,2,1,0:T(4,128)S(1)} %get-tuple-element.315, pred[1024,3072]{1,0:T(8,128)(4,1)} %iota_compare_fusion.4), kind=kLoop, calls=%fused_computation.7.clone.1 | loop fusion | flops 201310208 | bytes 204603392 | tf_op jit(solution)/shard_map/while/body/eval_jaxpr/reduce_sum | solution.py:83
  384.9 70.1 %bitcast_dynamic-update-slice_fusion.6 = bf16[3,2,1024,2,4,64]{2,5,4,3,1,0:T(8,128)(2,1)} fusion(bf16[3,2,1024,2,4,64]{2,5,4,3,1,0:T(8,128)(2,1)} %get-tuple-element.338, s32[]{:T(128)S(6)} %copy.89, f32[2,2,1024,4,3072]{4,2,3,1,0:T(8,128)} %get-tuple-element.314, f32[2,2,4,1024]{3,2,1,0:T(4,128)S(1)} %fusion.152, ...), kind=kOutput, calls=%fused_computation.10.clone.1 | convolution fusion | flops 6695157760 | bytes 208273408 | tf_op jit(solution)/shard_map/while/body/eval_jaxpr/bkgqt,btkd->bqkgd/dot_general | solution.py:85
  461.6 68.8 %bitcast_reduce_fusion.2 = (f32[2,2,4,1024]{3,2,1,0:T(4,128)S(1)}, f32[2,2,1024,4,3072]{4,2,3,1,0:T(8,128)}) fusion(pred[1024,3072]{1,0:T(8,128)(4,1)} %iota_compare_fusion.4, bf16[2,3072,2,64]{1,3,2,0:T(8,128)(2,1)} %get-tuple-element.353, bf16[2,3072,2,4,64]{1,4,3,2,0:T(8,128)(2,1)} %get-tuple-element.352, s32[]{:T(128)S(6)} %select_n.50), kind=kOutput, calls=%fused_computation.3.clone.2 | convolution fusion | flops 6593429504 | bytes 208207872 | tf_op jit(solution)/shard_map/while/body/eval_jaxpr/bqkgd,btkd->bkgqt/dot_general | solution.py:78
  530.3 63.0 %fusion.152 = f32[2,2,4,1024]{3,2,1,0:T(4,128)S(1)} fusion(f32[2,2,1024,4,3072]{4,2,3,1,0:T(8,128)} %get-tuple-element.314, f32[2,2,4,1024]{3,2,1,0:T(4,128)S(1)} %get-tuple-element.315, pred[1024,3072]{1,0:T(8,128)(4,1)} %iota_compare_fusion.4), kind=kLoop, calls=%fused_computation.7.clone.1 | loop fusion | flops 201310208 | bytes 204603392 | tf_op jit(solution)/shard_map/while/body/eval_jaxpr/reduce_sum | solution.py:83
  593.3 70.1 %bitcast_dynamic-update-slice_fusion.6 = bf16[3,2,1024,2,4,64]{2,5,4,3,1,0:T(8,128)(2,1)} fusion(bf16[3,2,1024,2,4,64]{2,5,4,3,1,0:T(8,128)(2,1)} %get-tuple-element.338, s32[]{:T(128)S(6)} %copy.89, f32[2,2,1024,4,3072]{4,2,3,1,0:T(8,128)} %get-tuple-element.314, f32[2,2,4,1024]{3,2,1,0:T(4,128)S(1)} %fusion.152, ...), kind=kOutput, calls=%fused_computation.10.clone.1 | convolution fusion | flops 6695157760 | bytes 208273408 | tf_op jit(solution)/shard_map/while/body/eval_jaxpr/bkgqt,btkd->bqkgd/dot_general | solution.py:85
  670.0 68.8 %bitcast_reduce_fusion.2 = (f32[2,2,4,1024]{3,2,1,0:T(4,128)S(1)}, f32[2,2,1024,4,3072]{4,2,3,1,0:T(8,128)}) fusion(pred[1024,3072]{1,0:T(8,128)(4,1)} %iota_compare_fusion.4, bf16[2,3072,2,64]{1,3,2,0:T(8,128)(2,1)} %get-tuple-element.353, bf16[2,3072,2,4,64]{1,4,3,2,0:T(8,128)(2,1)} %get-tuple-element.352, s32[]{:T(128)S(6)} %select_n.50), kind=kOutput, calls=%fused_computation.3.clone.2 | convolution fusion | flops 6593429504 | bytes 208207872 | tf_op jit(solution)/shard_map/while/body/eval_jaxpr/bqkgd,btkd->bkgqt/dot_general | solution.py:78
  738.7 63.0 %fusion.152 = f32[2,2,4,1024]{3,2,1,0:T(4,128)S(1)} fusion(f32[2,2,1024,4,3072]{4,2,3,1,0:T(8,128)} %get-tuple-element.314, f32[2,2,4,1024]{3,2,1,0:T(4,128)S(1)} %get-tuple-element.315, pred[1024,3072]{1,0:T(8,128)(4,1)} %iota_compare_fusion.4), kind=kLoop, calls=%fused_computation.7.clone.1 | loop fusion | flops 201310208 | bytes 204603392 | tf_op jit(solution)/shard_map/while/body/eval_jaxpr/reduce_sum | solution.py:83
  801.7 70.1 %bitcast_dynamic-update-slice_fusion.6 = bf16[3,2,1024,2,4,64]{2,5,4,3,1,0:T(8,128)(2,1)} fusion(bf16[3,2,1024,2,4,64]{2,5,4,3,1,0:T(8,128)(2,1)} %get-tuple-element.338, s32[]{:T(128)S(6)} %copy.89, f32[2,2,1024,4,3072]{4,2,3,1,0:T(8,128)} %get-tuple-element.314, f32[2,2,4,1024]{3,2,1,0:T(4,128)S(1)} %fusion.152, ...), kind=kOutput, calls=%fused_computation.10.clone.1 | convolution fusion | flops 6695157760 | bytes 208273408 | tf_op jit(solution)/shard_map/while/body/eval_jaxpr/bkgqt,btkd->bqkgd/dot_general | solution.py:85
  875.9 1632.4 %while.29 = (s32[]{:T(128)}, f32[2,3072,2,64]{1,3,2,0:T(8,128)}, f32[2,3072,2,64]{1,3,2,0:T(8,128)}, bf16[3,2,1024,2,4,64]{2,5,4,3,1,0:T(8,128)(2,1)}, s32[3]{0:...) while((s32[]{:T(128)}, f32[2,3072,2,64]{1,3,2,0:T(8,128)}, ...), condition=%wide.region_7.8_spmd.clone, body=%wide.region_5.7_spmd.clone.sunk | while | flops 33175937024 | bytes 1745559680 | solution.py:122
  882.4 37.4 %convolution_convert_fusion.2 = bf16[2,2,1024,4,3072]{4,2,3,1,0:T(8,128)(2,1)} fusion(bf16[2,3072,2,4,64]{1,4,3,2,0:T(8,128)(2,1)} %get-tuple-element.395, s32[]{:T(128)S(6)} %select_n.52, bf16[2,3072,2,64]{1,3,2,0:T(8,128)(2,1)} %get-tuple-element.396), kind=kOutput, calls=%fused_computation.31.clone.2 | convolution fusion | flops 6492782592 | bytes 104333312 | tf_op jit(solution)/shard_map/while/body/eval_jaxpr/bqkgd,btkd->bkgqt/dot_general | solution.py:113
  919.8 70.6 %fusion.161 = f32[2,2,4,1024,3072]{4,3,2,1,0:T(8,128)} fusion(f32[2,2,4,1024]{3,2,1,0:T(4,128)S(1)} %dynamic-slice_bitcast_fusion.2, pred[1024,3072]{1,0:T(8,128)(4,1)} %iota_compare_fusion.5, bf16[2,3072,2,4,64]{1,4,3,2,0:T(8,128)(2,1)} %get-tuple-element.392, s32[]{:T(128)S(6)} %select_n.52, bf16[2,3072,2,64]{1,3,2,0:T(8,128)(2,1)} %get-tuple-element.393), kind=kOutput, calls=%fused_computation.27.clone.2 | convolution fusion | flops 6593445888 | bytes 208207872 | tf_op jit(solution)/shard_map/while/body/eval_jaxpr/bqkgd,btkd->bkgqt/dot_general | solution.py:109
  990.4 63.2 %select_add_fusion.2 = f32[2,3072,2,64]{1,3,2,0:T(8,128)} fusion(f32[2,3072,2,64]{1,3,2,0:T(8,128)} %get-tuple-element.375, f32[2,2,4,1024,3072]{4,3,2,1,0:T(8,128)} %fusion.161, bf16[2,3072,2,4,64]{1,4,3,2,0:T(8,128)(2,1)} %get-tuple-element.395, s32[]{:T(128)S(6)} %select_n.52, pred[]{:T(512)S(6)} %compare.3), kind=kOutput, calls=%fused_computation.38.clone.2 | convolution fusion | flops 6494355456 | bytes 209715200 | tf_op jit(solution)/shard_map/while/body/eval_jaxpr/bkgqt,bqkgd->btkd/dot_general | solution.py:118
  1053.6 183.5 %fusion.162 = f32[2,3072,2,64]{1,3,2,0:T(8,128)} fusion(f32[2,2,4,1024,3072]{4,3,2,1,0:T(8,128)} %fusion.161, bf16[2,2,1024,4,3072]{4,2,3,1,0:T(8,128)(2,1)} %convolution_convert_fusion.2, f32[2,3072,2,64]{1,3,2,0:T(8,128)} %get-tuple-element.374, bf16[2,3072,2,4,64]{1,4,3,2,0:T(8,128)(2,1)} %get-tuple-element.392, s32[]{:T(128)S(6)} %select_n.52, ...), kind=kOutput, calls=%fused_computation.37.clone.2 | convolution fusion | flops 6796364800 | bytes 612368384 | tf_op jit(solution)/shard_map/while/body/eval_jaxpr/bkgqt,bqkgd->btkd/dot_general | solution.py:117
  1237.1 181.8 %bitcast_dynamic-update-slice_fusion.8 = bf16[3,2,1024,2,4,64]{2,5,4,3,1,0:T(8,128)(2,1)} fusion(bf16[3,2,1024,2,4,64]{2,5,4,3,1,0:T(8,128)(2,1)} %get-tuple-element.376, s32[]{:T(128)S(6)} %copy.99, f32[2,2,4,1024,3072]{4,3,2,1,0:T(8,128)} %fusion.161, bf16[2,2,1024,4,3072]{4,2,3,1,0:T(8,128)(2,1)} %convolution_convert_fusion.2, ...), kind=kOutput, calls=%fused_computation.39.clone.1 | convolution fusion | flops 6795840512 | bytes 607649792 | tf_op jit(solution)/shard_map/while/body/eval_jaxpr/bkgqt,btkd->bqkgd/dot_general | solution.py:116
  1425.2 37.4 %convolution_convert_fusion.2 = bf16[2,2,1024,4,3072]{4,2,3,1,0:T(8,128)(2,1)} fusion(bf16[2,3072,2,4,64]{1,4,3,2,0:T(8,128)(2,1)} %get-tuple-element.395, s32[]{:T(128)S(6)} %select_n.52, bf16[2,3072,2,64]{1,3,2,0:T(8,128)(2,1)} %get-tuple-element.396), kind=kOutput, calls=%fused_computation.31.clone.2 | convolution fusion | flops 6492782592 | bytes 104333312 | tf_op jit(solution)/shard_map/while/body/eval_jaxpr/bqkgd,btkd->bkgqt/dot_general | solution.py:113
  1462.7 70.6 %fusion.161 = f32[2,2,4,1024,3072]{4,3,2,1,0:T(8,128)} fusion(f32[2,2,4,1024]{3,2,1,0:T(4,128)S(1)} %dynamic-slice_bitcast_fusion.2, pred[1024,3072]{1,0:T(8,128)(4,1)} %iota_compare_fusion.5, bf16[2,3072,2,4,64]{1,4,3,2,0:T(8,128)(2,1)} %get-tuple-element.392, s32[]{:T(128)S(6)} %select_n.52, bf16[2,3072,2,64]{1,3,2,0:T(8,128)(2,1)} %get-tuple-element.393), kind=kOutput, calls=%fused_computation.27.clone.2 | convolution fusion | flops 6593445888 | bytes 208207872 | tf_op jit(solution)/shard_map/while/body/eval_jaxpr/bqkgd,btkd->bkgqt/dot_general | solution.py:109
  1533.2 64.2 %select_add_fusion.2 = f32[2,3072,2,64]{1,3,2,0:T(8,128)} fusion(f32[2,3072,2,64]{1,3,2,0:T(8,128)} %get-tuple-element.375, f32[2,2,4,1024,3072]{4,3,2,1,0:T(8,128)} %fusion.161, bf16[2,3072,2,4,64]{1,4,3,2,0:T(8,128)(2,1)} %get-tuple-element.395, s32[]{:T(128)S(6)} %select_n.52, pred[]{:T(512)S(6)} %compare.3), kind=kOutput, calls=%fused_computation.38.clone.2 | convolution fusion | flops 6494355456 | bytes 209715200 | tf_op jit(solution)/shard_map/while/body/eval_jaxpr/bkgqt,bqkgd->btkd/dot_general | solution.py:118
  1597.5 184.3 %fusion.162 = f32[2,3072,2,64]{1,3,2,0:T(8,128)} fusion(f32[2,2,4,1024,3072]{4,3,2,1,0:T(8,128)} %fusion.161, bf16[2,2,1024,4,3072]{4,2,3,1,0:T(8,128)(2,1)} %convolution_convert_fusion.2, f32[2,3072,2,64]{1,3,2,0:T(8,128)} %get-tuple-element.374, bf16[2,3072,2,4,64]{1,4,3,2,0:T(8,128)(2,1)} %get-tuple-element.392, s32[]{:T(128)S(6)} %select_n.52, ...), kind=kOutput, calls=%fused_computation.37.clone.2 | convolution fusion | flops 6796364800 | bytes 612368384 | tf_op jit(solution)/shard_map/while/body/eval_jaxpr/bkgqt,bqkgd->btkd/dot_general | solution.py:117
  1781.8 181.8 %bitcast_dynamic-update-slice_fusion.8 = bf16[3,2,1024,2,4,64]{2,5,4,3,1,0:T(8,128)(2,1)} fusion(bf16[3,2,1024,2,4,64]{2,5,4,3,1,0:T(8,128)(2,1)} %get-tuple-element.376, s32[]{:T(128)S(6)} %copy.99, f32[2,2,4,1024,3072]{4,3,2,1,0:T(8,128)} %fusion.161, bf16[2,2,1024,4,3072]{4,2,3,1,0:T(8,128)(2,1)} %convolution_convert_fusion.2, ...), kind=kOutput, calls=%fused_computation.39.clone.1 | convolution fusion | flops 6795840512 | bytes 607649792 | tf_op jit(solution)/shard_map/while/body/eval_jaxpr/bkgqt,btkd->bqkgd/dot_general | solution.py:116
  1969.9 37.4 %convolution_convert_fusion.2 = bf16[2,2,1024,4,3072]{4,2,3,1,0:T(8,128)(2,1)} fusion(bf16[2,3072,2,4,64]{1,4,3,2,0:T(8,128)(2,1)} %get-tuple-element.395, s32[]{:T(128)S(6)} %select_n.52, bf16[2,3072,2,64]{1,3,2,0:T(8,128)(2,1)} %get-tuple-element.396), kind=kOutput, calls=%fused_computation.31.clone.2 | convolution fusion | flops 6492782592 | bytes 104333312 | tf_op jit(solution)/shard_map/while/body/eval_jaxpr/bqkgd,btkd->bkgqt/dot_general | solution.py:113
  2007.3 70.6 %fusion.161 = f32[2,2,4,1024,3072]{4,3,2,1,0:T(8,128)} fusion(f32[2,2,4,1024]{3,2,1,0:T(4,128)S(1)} %dynamic-slice_bitcast_fusion.2, pred[1024,3072]{1,0:T(8,128)(4,1)} %iota_compare_fusion.5, bf16[2,3072,2,4,64]{1,4,3,2,0:T(8,128)(2,1)} %get-tuple-element.392, s32[]{:T(128)S(6)} %select_n.52, bf16[2,3072,2,64]{1,3,2,0:T(8,128)(2,1)} %get-tuple-element.393), kind=kOutput, calls=%fused_computation.27.clone.2 | convolution fusion | flops 6593445888 | bytes 208207872 | tf_op jit(solution)/shard_map/while/body/eval_jaxpr/bqkgd,btkd->bkgqt/dot_general | solution.py:109
  2077.9 64.1 %select_add_fusion.2 = f32[2,3072,2,64]{1,3,2,0:T(8,128)} fusion(f32[2,3072,2,64]{1,3,2,0:T(8,128)} %get-tuple-element.375, f32[2,2,4,1024,3072]{4,3,2,1,0:T(8,128)} %fusion.161, bf16[2,3072,2,4,64]{1,4,3,2,0:T(8,128)(2,1)} %get-tuple-element.395, s32[]{:T(128)S(6)} %select_n.52, pred[]{:T(512)S(6)} %compare.3), kind=kOutput, calls=%fused_computation.38.clone.2 | convolution fusion | flops 6494355456 | bytes 209715200 | tf_op jit(solution)/shard_map/while/body/eval_jaxpr/bkgqt,bqkgd->btkd/dot_general | solution.py:118
  2142.0 184.2 %fusion.162 = f32[2,3072,2,64]{1,3,2,0:T(8,128)} fusion(f32[2,2,4,1024,3072]{4,3,2,1,0:T(8,128)} %fusion.161, bf16[2,2,1024,4,3072]{4,2,3,1,0:T(8,128)(2,1)} %convolution_convert_fusion.2, f32[2,3072,2,64]{1,3,2,0:T(8,128)} %get-tuple-element.374, bf16[2,3072,2,4,64]{1,4,3,2,0:T(8,128)(2,1)} %get-tuple-element.392, s32[]{:T(128)S(6)} %select_n.52, ...), kind=kOutput, calls=%fused_computation.37.clone.2 | convolution fusion | flops 6796364800 | bytes 612368384 | tf_op jit(solution)/shard_map/while/body/eval_jaxpr/bkgqt,bqkgd->btkd/dot_general | solution.py:117
  2326.2 181.8 %bitcast_dynamic-update-slice_fusion.8 = bf16[3,2,1024,2,4,64]{2,5,4,3,1,0:T(8,128)(2,1)} fusion(bf16[3,2,1024,2,4,64]{2,5,4,3,1,0:T(8,128)(2,1)} %get-tuple-element.376, s32[]{:T(128)S(6)} %copy.99, f32[2,2,4,1024,3072]{4,3,2,1,0:T(8,128)} %fusion.161, bf16[2,2,1024,4,3072]{4,2,3,1,0:T(8,128)(2,1)} %convolution_convert_fusion.2, ...), kind=kOutput, calls=%fused_computation.39.clone.1 | convolution fusion | flops 6795840512 | bytes 607649792 | tf_op jit(solution)/shard_map/while/body/eval_jaxpr/bkgqt,btkd->bqkgd/dot_general | solution.py:116
  2552.7 19.9 copy.78
  2572.6 12.8 reshape.173
  2590.7 19.9 copy.76
  2610.6 12.8 reshape.167
  2639.3 21.7 all-to-all-done.5
  2697.4 12.7 reshape.174
  2710.1 14.9 copy.79
  2736.7 12.7 reshape.168
  2749.4 15.1 copy.77
  2768.6 22.1 convolution_bitcast_fusion
  2790.7 18.3 convolution_bitcast_fusion.1
  2831.8 25.4 fusion.56
  2864.5 12.5 fusion.53
  2877.1 18.1 fusion.58
  2895.1 603.5 %all-reduce.3.cloned.1.call-done = (f32[2048,32,64]{0,2,1:T(8,128)}, f32[2048,8,64]{0,2,1:T(8,128)}, f32[2048,8,64]{0,2,1:T(8,128)}, f32[32,64,2048]{2,1,0:T(8,128)}) async-done(((f32[2048,32,64]{0,2,1:T(8,128)}, f32[2048,8,64]{0,2,1:T(8,128)}, f32[2048,8,64]{0,2,1:T(8,128)}, f32[32,64,2048]{2,1,0:T(8,128)}), (f32[2048,32,64]{0,2,1:T(8,128)}, f32[2048,8,64]{0,2,1:T(8,128)}, f32[2048,8,64]{0,2,1:T(8,128)}, ...) | async-done | bytes 41943056 | tf_op jit(solution)/shard_map/psum | solution.py:168
  3498.7 13.6 copy.111
  (171 shorter events, 306.5 us)
Async XLA Ops:
  7.2 15.8 copy-start
  7.2 4.8 copy-start.1
  7.2 4.7 copy-start.19
  11.9 62.2 %copy-start.17 = (f32[2,768]{1,0:T(2,128)}, f32[2,768]{1,0:T(2,128)S(1)}, u32[]{:S(2)}) copy-start(f32[2,768]{1,0:T(2,128)S(1)} %add_rsqrt_fusion) | copy-start | bytes 18436
  18.4 25.2 all-to-all-start.2
  31.4 60.4 %copy-start.8 = (f32[768,32]{0,1:T(8,128)}, f32[768,32]{0,1:T(8,128)S(1)}, u32[]{:S(2)}) copy-start(f32[768,32]{0,1:T(8,128)S(1)} %get-tuple-element.215) | copy-start | bytes 294916
  31.4 60.4 %copy-start.11 = (f32[768,32]{0,1:T(8,128)}, f32[768,32]{0,1:T(8,128)S(1)}, u32[]{:S(2)}) copy-start(f32[768,32]{0,1:T(8,128)S(1)} %get-tuple-element.216) | copy-start | bytes 294916
  43.6 25.3 all-to-all-start.1
  68.8 75.7 %all-to-all-start.4 = ((bf16[2,768,32,64]{1,3,0,2:T(8,128)(2,1)}), bf16[2,768,32,64]{1,3,0,2:T(8,128)(2,1)}, u32[]{:S(2)}, u32[]{:S(2)}) async-start(bf16[2,768,32,64]{1,3,0,2:T(8,128)(2,1)} %copy.48), calls=%async_computation.4 | async-start | bytes 12582912 | tf_op jit(solution)/shard_map/all_to_all | solution.py:151
  144.5 75.8 %all-to-all-start = ((bf16[2,768,32,64]{1,3,0,2:T(8,128)(2,1)}), bf16[2,768,32,64]{1,3,0,2:T(8,128)(2,1)}, u32[]{:S(2)}, u32[]{:S(2)}) async-start(bf16[2,768,32,64]{1,3,0,2:T(8,128)(2,1)} %copy.38), calls=%async_computation | async-start | bytes 12582912 | tf_op jit(solution)/shard_map/all_to_all | solution.py:142
  876.1 1.3 copy-start.22
  1237.1 181.8 %copy-start.23 = (s32[3]{0:T(128)S(1)}, s32[3]{0:T(128)}, u32[]{:S(2)}) copy-start(s32[3]{0:T(128)} %copy-done.22) | copy-start | bytes 40 | tf_op jit(solution)/shard_map/while
  1418.9 1.3 copy-start.22
  1781.8 181.8 %copy-start.23 = (s32[3]{0:T(128)S(1)}, s32[3]{0:T(128)}, u32[]{:S(2)}) copy-start(s32[3]{0:T(128)} %copy-done.22) | copy-start | bytes 40 | tf_op jit(solution)/shard_map/while
  1963.6 1.3 copy-start.22
  2326.2 181.8 %copy-start.23 = (s32[3]{0:T(128)S(1)}, s32[3]{0:T(128)}, u32[]{:S(2)}) copy-start(s32[3]{0:T(128)} %copy-done.22) | copy-start | bytes 40 | tf_op jit(solution)/shard_map/while
  2524.2 24.1 all-to-all-start.6
  2548.3 37.1 %all-to-all-start.7 = ((bf16[4,2,98304]{2,1,0:T(2,128)(2,1)}), bf16[4,2,98304]{2,1,0:T(2,128)(2,1)}, u32[]{:S(2)}, u32[]{:S(2)}) async-start(bf16[4,2,98304]{2,1,0:T(2,128)(2,1)} %reshape.169), calls=%async_computation.7 | async-start | bytes 3145728 | tf_op jit(solution)/shard_map/all_to_all | solution.py:155
  2585.4 75.6 %all-to-all-start.5 = ((bf16[4,2,393216]{2,1,0:T(2,128)(2,1)}), bf16[4,2,393216]{2,1,0:T(2,128)(2,1)}, u32[]{:S(2)}, u32[]{:S(2)}) async-start(bf16[4,2,393216]{2,1,0:T(2,128)(2,1)} %reshape.173), calls=%async_computation.5 | async-start | bytes 12582912 | tf_op jit(solution)/shard_map/all_to_all | solution.py:153
  2623.4 13.1 copy-start.9
  2623.4 13.1 copy-start.12
  2639.3 27.1 copy-start.15
  2639.3 27.1 copy-start.18
  2639.3 27.1 copy-start.20
  2661.1 75.6 %all-to-all-start.3 = ((bf16[4,2,393216]{2,1,0:T(2,128)(2,1)}), bf16[4,2,393216]{2,1,0:T(2,128)(2,1)}, u32[]{:S(2)}, u32[]{:S(2)}) async-start(bf16[4,2,393216]{2,1,0:T(2,128)(2,1)} %reshape.167), calls=%async_computation.3 | async-start | bytes 12582912 | tf_op jit(solution)/shard_map/all_to_all | solution.py:146
  2666.3 832.3 %all-reduce.3.cloned.1.call-start = ((), (), s32[]{:S(2)}) async-start(), calls=%async_computation.8 | async-start | bytes 83886080 | tf_op jit(solution)/shard_map/psum | solution.py:168
  2725.0 4.0 copy-start.10
  2725.0 4.0 copy-start.13
  2764.4 26.2 slice-start
  2768.6 22.1 copy-start.2
  2768.6 22.1 slice-start.1
  2768.6 22.1 copy-start.5
  2768.6 22.1 copy-start.7
  2809.0 8.3 copy-start.16
  2817.3 8.2 copy-start.14
  2817.3 8.2 copy-start.21
  2825.4 6.4 copy-start.6
  2864.5 12.6 slice-start.2
  2864.5 12.6 slice-start.8
  2864.5 12.5 slice-start.3
  2864.5 12.5 slice-start.9
  3498.7 13.6 copy-start.4
  3498.7 20.3 slice-start.4
  3498.7 20.3 slice-start.5
  3498.7 20.3 slice-start.6
  3512.2 4.6 copy-start.3
  3512.2 8.5 slice-start.7
Sparse Core Ops, SparseCore 0:
  2809.1 689.4 all-reduce.2
where the time goes:
time: 3550 us; the launch traced here: 3530 us
  matrix products  2190 us (62%)
  waiting for transfers between devices  717 us (20%)
  local copies, waits for them, and re-layouts  303 us (9%)
  other arithmetic  254 us (7%)
  starting transfers between devices  39.4 us (1%)
    psum x1, waiting for transfers between devices, local_step(): lax.psum((d_wq, d_wk, d_wv, d_wo, d_gain), 'sp')  604 us
    dot_general x3, matrix products, one_block(): jnp.einsum('bkgqt,bqkgd->btkd', d_scores, q_rows, preferred_element_type=...  552 us
    dot_general x3, matrix products, one_block(): jnp.einsum('bkgqt,btkd->bqkgd', d_scores, k_heads, preferred_element_type...  545 us
    dot_general x6, matrix products, one_block(): jnp.einsum('bqkgd,btkd->bkgqt', q_rows, k_heads, preferred_element_type=j...  418 us
    dot_general x3, matrix products, one_block(): jnp.einsum('bkgqt,btkd->bqkgd', attn_weights, v_heads, preferred_element_...  210 us
    dot_general x3, matrix products, one_block(): jnp.einsum('bkgqt,bqkgd->btkd', attn_weights.astype(jnp.bfloat16), d_rows...  191 us
    reduce_sum x3, other arithmetic, one_block(): row_sum = jnp.sum(exp_scores, axis=-1, keepdims=True)  189 us
    dot_general x3, matrix products, one_block(): jnp.einsum('bqkgd,btkd->bkgqt', d_rows, v_heads, preferred_element_type=j...  112 us
  transfers between devices with their start and end apart: 9, of which 7 were waited for; matrix products, arithmetic and copies ran while one was open for 9% of the time, Pallas kernels for 0%

commit v1 on v0

v1 whole, which is shorter than its diff:
```python
import jax
import jax.numpy as jnp
from jax import lax
from jax.experimental import pallas as pl
from jax.experimental.pallas import tpu as pltpu
from jax.sharding import PartitionSpec as P

ROPE_BASE = 1000000.0
NORM_EPS = 1e-5
HD = 64
GROUP = 4
BQ = 256
WIDE = 512
LOG2E = 1.4426950408889634
NEG = -1e30


def causal_steps(step, q_idx):
    per_wide = WIDE // BQ

    def body(i, carry):
        step(pl.multiple_of(i * WIDE, WIDE), WIDE, False)
        return carry

    wide = q_idx // per_wide
    lax.fori_loop(0, wide, body, 0)

    def tail(i, carry):
        step(pl.multiple_of(i * BQ, BQ), BQ, False)
        return carry

    lax.fori_loop(wide * per_wide, q_idx, tail, 0)
    step(pl.multiple_of(q_idx * BQ, BQ), BQ, True)


def mask_scores(scores):
    rows = lax.broadcasted_iota(jnp.int32, scores.shape, 0)
    cols = lax.broadcasted_iota(jnp.int32, scores.shape, 1)
    return jnp.where(rows <= cols, scores, NEG)


def transpose_rows(src_ref, dst_ref):
    seq = dst_ref.shape[0]

    def body(i, carry):
        start = pl.multiple_of(i * WIDE, WIDE)
        dst_ref[pl.ds(start, WIDE), :] = src_ref[:, pl.ds(start, WIDE)].T
        return carry

    lax.fori_loop(0, seq // WIDE, body, 0)


def fwd_kernel(qt_ref, kt_ref, vt_ref, ot_ref, lse_ref, k_scr, acc_scr, m_scr, l_scr):
    q_idx = pl.program_id(1)

    @pl.when(q_idx == 0)
    def _():
        transpose_rows(kt_ref, k_scr)

    acc_scr[...] = jnp.zeros_like(acc_scr)
    m_scr[...] = jnp.full_like(m_scr, NEG)
    l_scr[...] = jnp.zeros_like(l_scr)
    factor = HD ** -0.5 * LOG2E

    def step(start, width, masked):
        k_rows = k_scr[pl.ds(start, width), :]
        v_cols = vt_ref[:, pl.ds(start, width)]
        m_all = m_scr[...]
        l_all = l_scr[...]
        scores = [jnp.dot(k_rows, qt_ref[g * HD:(g + 1) * HD, :], preferred_element_type=jnp.float32) for g in range(GROUP)]
        if masked:
            scores = [mask_scores(s) for s in scores]
        m_new, l_new, accs = [], [], []
        for g in range(GROUP):
            m_prev = m_all[g:g + 1]
            peak = jnp.maximum(m_prev, jnp.max(scores[g], axis=0, keepdims=True) * factor)
            probs = jnp.exp2(scores[g] * factor - peak)
            alpha = jnp.exp2(m_prev - peak)
            l_new.append(l_all[g:g + 1] * alpha + jnp.sum(probs, axis=0, keepdims=True))
            m_new.append(peak)
            accs.append(acc_scr[g * HD:(g + 1) * HD, :] * alpha + jnp.dot(v_cols, probs.astype(jnp.bfloat16), preferred_element_type=jnp.float32))
        for g in range(GROUP):
            m_scr[g:g + 1, :] = m_new[g]
            l_scr[g:g + 1, :] = l_new[g]
            acc_scr[g * HD:(g + 1) * HD, :] = accs[g]

    causal_steps(step, q_idx)
    lse_ref[0] = m_scr[...] + jnp.log2(jnp.maximum(l_scr[...], 1e-30))
    for g in range(GROUP):
        heads = slice(g * HD, (g + 1) * HD)
        ot_ref[0, heads, :] = (acc_scr[heads, :] / l_scr[g:g + 1, :]).astype(jnp.bfloat16)


def bwd_kernel(qt_ref, kt_ref, vt_ref, dot_ref, ot_ref, lse_ref, cosq_ref, sinq_ref, cos_ref, sin_ref, dqt_ref, dkt_ref, dvt_ref, k_scr, v_scr, dk_scr, dv_scr, dq_scr, q_scr, do_scr, dos_scr, delta_scr):
    q_idx = pl.program_id(1)
    seq = k_scr.shape[0]

    @pl.when(q_idx == 0)
    def _():
        transpose_rows(kt_ref, k_scr)
        transpose_rows(vt_ref, v_scr)
        dk_scr[...] = jnp.zeros_like(dk_scr)
        dv_scr[...] = jnp.zeros_like(dv_scr)

    dq_scr[...] = jnp.zeros_like(dq_scr)
    scale = HD ** -0.5
    factor = scale * LOG2E
    for g in range(GROUP):
        heads = slice(g * HD, (g + 1) * HD)
        do_t = dot_ref[heads, :]
        q_scr[g] = qt_ref[heads, :].T
        do_scr[g] = do_t.T
        do_f32 = do_t.astype(jnp.float32) * scale
        dos_scr[heads, :] = do_f32.astype(jnp.bfloat16)
        delta_scr[g:g + 1, :] = jnp.sum(do_f32 * ot_ref[0, heads, :].astype(jnp.float32), axis=0, keepdims=True)

    def step(start, width, masked):
        rows = pl.ds(start, width)
        k_rows = k_scr[rows, :]
        v_rows = v_scr[rows, :]
        k_cols = kt_ref[:, rows]
        dk_sum = dv_sum = None
        for g in range(GROUP):
            heads = slice(g * HD, (g + 1) * HD)
            scores = jnp.dot(k_rows, qt_ref[heads, :], preferred_element_type=jnp.float32) * factor
            if masked:
                scores = mask_scores(scores)
            probs = jnp.exp2(scores - lse_ref[0, g:g + 1, :])
            d_probs = jnp.dot(v_rows, dos_scr[heads, :], preferred_element_type=jnp.float32).astype(jnp.bfloat16).astype(jnp.float32)
            d_scores = (probs * (d_probs - delta_scr[g:g + 1, :])).astype(jnp.bfloat16)
            dv_part = jnp.dot(probs.astype(jnp.bfloat16), do_scr[g], preferred_element_type=jnp.float32)
            dk_part = jnp.dot(d_scores, q_scr[g], preferred_element_type=jnp.float32)
            dv_sum = dv_part if g == 0 else dv_sum + dv_part
            dk_sum = dk_part if g == 0 else dk_sum + dk_part
            dq_scr[heads, :] = dq_scr[heads, :] + jnp.dot(k_cols, d_scores, preferred_element_type=jnp.float32)
        dv_scr[rows, :] = dv_scr[rows, :] + dv_sum
        dk_scr[rows, :] = dk_scr[rows, :] + dk_sum

    causal_steps(step, q_idx)
    half = HD // 2
    cos_q = cosq_ref[...]
    sin_q = sinq_ref[...]
    for g in range(GROUP):
        grad = dq_scr[g * HD:(g + 1) * HD, :].astype(jnp.bfloat16).astype(jnp.float32)
        first, second = grad[:half], grad[half:]
        dqt_ref[0, g * HD:g * HD + half, :] = (first * cos_q + second * sin_q).astype(jnp.bfloat16)
        dqt_ref[0, g * HD + half:(g + 1) * HD, :] = (second * cos_q - first * sin_q).astype(jnp.bfloat16)

    @pl.when(q_idx == pl.num_programs(1) - 1)
    def _():
        per = dkt_ref.shape[2]
        for j in range(seq // per):
            cols = slice(j * per, (j + 1) * per)
            grad = dk_scr[cols, :].T.astype(jnp.bfloat16).astype(jnp.float32)
            first, second = grad[:half], grad[half:]
            dkt_ref[j, :half, :] = (first * cos_ref[:, cols] + second * sin_ref[:, cols]).astype(jnp.bfloat16)
            dkt_ref[j, half:, :] = (second * cos_ref[:, cols] - first * sin_ref[:, cols]).astype(jnp.bfloat16)
            dvt_ref[j] = dv_scr[cols, :].T.astype(jnp.bfloat16)


def attn_fwd(qt, kt, vt, parts):
    feats, seq = qt.shape
    num_kv = kt.shape[0] // HD
    per = seq // parts
    sub = per // BQ
    rows = GROUP * HD
    pairs = num_kv * GROUP * seq * seq // 2
    return pl.pallas_call(
        fwd_kernel,
        grid=(num_kv, seq // BQ),
        in_specs=[
            pl.BlockSpec((rows, BQ), lambda h, i: (h, i)),
            pl.BlockSpec((HD, seq), lambda h, i: (h, 0)),
            pl.BlockSpec((HD, seq), lambda h, i: (h, 0)),
        ],
        out_specs=[
            pl.BlockSpec((1, rows, BQ), lambda h, i: (i // sub, h, i % sub)),
            pl.BlockSpec((1, 8, BQ), lambda h, i: (h, 0, i)),
        ],
        out_shape=[
            jax.ShapeDtypeStruct((parts, feats, per), jnp.bfloat16),
            jax.ShapeDtypeStruct((num_kv, 8, seq), jnp.float32),
        ],
        scratch_shapes=[
            pltpu.VMEM((seq, HD), jnp.bfloat16),
            pltpu.VMEM((rows, BQ), jnp.float32),
            pltpu.VMEM((8, BQ), jnp.float32),
            pltpu.VMEM((8, BQ), jnp.float32),
        ],
        compiler_params=pltpu.CompilerParams(dimension_semantics=("arbitrary", "arbitrary"), vmem_limit_bytes=40 * 2 ** 20),
        cost_estimate=pl.CostEstimate(flops=pairs * 4 * 256, bytes_accessed=feats * seq * 6, transcendentals=pairs),
        name="attn_fwd",
    )(qt, kt, vt)


def attn_bwd(qt, kt, vt, dot, ot, lse, cos_t, sin_t):
    feats, seq = qt.shape
    num_kv = kt.shape[0] // HD
    parts, _, per = ot.shape
    sub = per // BQ
    rows = GROUP * HD
    half = HD // 2
    pairs = num_kv * GROUP * seq * seq // 2
    q_spec = pl.BlockSpec((rows, BQ), lambda h, i: (h, i))
    kv_spec = pl.BlockSpec((HD, seq), lambda h, i: (h, 0))
    part_spec = pl.BlockSpec((1, rows, BQ), lambda h, i: (i // sub, h, i % sub))
    rope_q = pl.BlockSpec((half, BQ), lambda h, i: (0, i))
    rope_all = pl.BlockSpec((half, seq), lambda h, i: (0, 0))
    dkv_spec = pl.BlockSpec((parts, HD, per), lambda h, i: (0, h, 0))
    return pl.pallas_call(
        bwd_kernel,
        grid=(num_kv, seq // BQ),
        in_specs=[q_spec, kv_spec, kv_spec, q_spec, part_spec, pl.BlockSpec((1, 8, BQ), lambda h, i: (h, 0, i)), rope_q, rope_q, rope_all, rope_all],
        out_specs=[part_spec, dkv_spec, dkv_spec],
        out_shape=[
            jax.ShapeDtypeStruct((parts, feats, per), jnp.bfloat16),
            jax.ShapeDtypeStruct((parts, num_kv * HD, per), jnp.bfloat16),
            jax.ShapeDtypeStruct((parts, num_kv * HD, per), jnp.bfloat16),
        ],
        scratch_shapes=[
            pltpu.VMEM((seq, HD), jnp.bfloat16),
            pltpu.VMEM((seq, HD), jnp.bfloat16),
            pltpu.VMEM((seq, HD), jnp.float32),
            pltpu.VMEM((seq, HD), jnp.float32),
            pltpu.VMEM((rows, BQ), jnp.float32),
            pltpu.VMEM((GROUP, BQ, HD), jnp.bfloat16),
            pltpu.VMEM((GROUP, BQ, HD), jnp.bfloat16),
            pltpu.VMEM((rows, BQ), jnp.bfloat16),
            pltpu.VMEM((8, BQ), jnp.float32),
        ],
        compiler_params=pltpu.CompilerParams(dimension_semantics=("arbitrary", "arbitrary"), vmem_limit_bytes=48 * 2 ** 20),
        cost_estimate=pl.CostEstimate(flops=pairs * 10 * 256, bytes_accessed=feats * seq * 10, transcendentals=pairs),
        name="attn_bwd",
    )(qt, kt, vt, dot, ot, lse, cos_t, sin_t, cos_t, sin_t)


def rope_tables(seq, head_dim):
    half = head_dim // 2
    inv_freq = ROPE_BASE ** (-2.0 * jnp.arange(half, dtype=jnp.float32) / head_dim)
    angle = inv_freq[:, None] * jnp.arange(seq, dtype=jnp.float32)[None, :]
    return jnp.cos(angle), jnp.sin(angle)


def rotate(lin, cos_t, sin_t):
    feats, seq = lin.shape
    half = HD // 2
    pairs = lin.reshape(feats // HD, 2, half, seq)
    first, second = pairs[:, 0], pairs[:, 1]
    turned = jnp.stack([first * cos_t - second * sin_t, second * cos_t + first * sin_t], axis=1)
    return turned.reshape(feats, seq).astype(jnp.bfloat16)


def dot32(spec, lhs, rhs):
    return jnp.einsum(spec, lhs, rhs, preferred_element_type=jnp.float32)


def solution(mesh):
    parts = mesh.shape['sp']

    def local_step(x_local, dy_local, gain, w_q, w_k, w_v, w_o):
        batch, seq_loc, d_model = x_local.shape
        seq = seq_loc * parts
        q_feats = w_q.shape[1] * HD // parts
        kv_feats = w_k.shape[1] * HD // parts
        idx = lax.axis_index('sp')

        def own(w):
            heads = w.shape[1] // parts
            return lax.dynamic_slice_in_dim(w, idx * heads, heads, axis=1).reshape(d_model, heads * HD)

        x_f32 = x_local.astype(jnp.float32)
        inv_rms = lax.rsqrt(jnp.mean(x_f32 * x_f32, axis=-1, keepdims=True) + NORM_EPS)
        normed = (x_f32 * inv_rms * gain).astype(jnp.bfloat16)

        r_all = [lax.all_gather(normed[b], 'sp', axis=0, tiled=True) for b in range(batch)]
        dy_all = [lax.all_gather(dy_local[b], 'sp', axis=0, tiled=True) for b in range(batch)]

        w_own = jnp.concatenate([own(w_q), own(w_k), own(w_v)], axis=1)
        w_cat = jnp.concatenate([w.reshape(d_model, parts, -1) for w in (w_q, w_k, w_v)], axis=2)
        w_o2 = w_o.reshape(parts, q_feats, d_model)
        w_o_own = lax.dynamic_index_in_dim(w_o2, idx, axis=0, keepdims=False)
        cos_t, sin_t = rope_tables(seq, HD)

        qkv, outs, y_rows = [], [], []
        for b in range(batch):
            lin = dot32('df,td->ft', w_own, r_all[b])
            q_t = rotate(lin[:q_feats], cos_t, sin_t)
            k_t = rotate(lin[q_feats:q_feats + kv_feats], cos_t, sin_t)
            v_t = lin[q_feats + kv_feats:].astype(jnp.bfloat16)
            o_t, lse = attn_fwd(q_t, k_t, v_t, parts)
            qkv.append((q_t, k_t, v_t))
            outs.append((o_t, lse))
            o_all = lax.all_to_all(o_t, 'sp', 0, 0, tiled=True)
            y_rows.append(dot32('jft,jfd->td', o_all, w_o2))
        y_out = (x_f32 + jnp.stack(y_rows)).astype(jnp.bfloat16)

        d_wo = None
        d_wqkv = None
        d_rows = []
        for b in range(batch):
            o_t, lse = outs[b]
            dy_parts = dy_all[b].reshape(parts, seq_loc, d_model)
            part = dot32('jft,jtd->fd', o_t, dy_parts)
            d_wo = part if d_wo is None else d_wo + part
        d_wo = lax.all_gather(d_wo, 'sp', axis=0, tiled=True)
        for b in range(batch):
            o_t, lse = outs[b]
            do_t = dot32('fd,td->ft', w_o_own, dy_all[b]).astype(jnp.bfloat16)
            grads = attn_bwd(*qkv[b], do_t, o_t, lse, cos_t, sin_t)
            d_qkv = jnp.concatenate(grads, axis=1)
            d_all = lax.all_to_all(d_qkv, 'sp', 0, 0, tiled=True)
            d_rows.append(dot32('jft,djf->td', d_all, w_cat))
            part = dot32('jtd,jft->df', r_all[b].reshape(parts, seq_loc, d_model), d_qkv)
            d_wqkv = part if d_wqkv is None else d_wqkv + part
        d_wqkv = lax.all_gather(d_wqkv, 'sp', axis=0)
        d_wqkv = jnp.moveaxis(d_wqkv, 0, 1)
        d_wq = d_wqkv[:, :, :q_feats].reshape(d_model, -1, HD)
        d_wk = d_wqkv[:, :, q_feats:q_feats + kv_feats].reshape(d_model, -1, HD)
        d_wv = d_wqkv[:, :, q_feats + kv_feats:].reshape(d_model, -1, HD)

        d_normed = jnp.stack(d_rows).astype(jnp.bfloat16).astype(jnp.float32)
        x_hat = x_f32 * inv_rms
        d_hat = d_normed * gain
        d_norm = inv_rms * (d_hat - x_hat * jnp.mean(d_hat * x_hat, axis=-1, keepdims=True))
        d_x = (dy_local.astype(jnp.float32) + d_norm).astype(jnp.bfloat16)
        d_gain = lax.psum(jnp.sum(d_normed * x_hat, axis=(0, 1)), 'sp')
        return y_out, d_x, d_wq, d_wk, d_wv, d_wo.reshape(-1, HD, d_model), d_gain

    specs_in = (P('dp', 'sp', None), P('dp', 'sp', None), P(None), P(None, None, None), P(None, None, None), P(None, None, None), P(None, None, None))
    specs_out = (P('dp', 'sp', None), P('dp', 'sp', None), P('dp', None, None), P('dp', None, None), P('dp', None, None), P('dp', None, None), P('dp'))
    return jax.shard_map(local_step, mesh=mesh, in_specs=specs_in, out_specs=specs_out, check_vma=False)
```

time: 3550 us -> 1170 us (0.33)
  matrix products: 2190 us -> 165 us
  waiting for transfers between devices: 717 us -> 240 us
  Pallas kernels: 0 us -> 441 us
  other arithmetic: 254 us -> 36.6 us
  local copies, waits for them, and re-layouts: 303 us -> 109 us
  blocking collectives: 7.28 us -> 148 us
    dot_general x33 -> x12, matrix products: 2190 us -> 165 us  [dot32(): return jnp.einsum(spec, lhs, rhs, preferred_element_type=jnp.float32)]
    psum x1 -> x0, waiting for transfers between devices: 604 us -> none  [local_step(): lax.psum((d_wq, d_wk, d_wv, d_wo, d_gain), 'sp')]
    pallas_call x0 -> x4, Pallas kernels: none -> 441 us  [the longest x2 277 us: attn_bwd(): pl.pallas_call(bwd_kernel, grid=(num_kv, seq // BQ), in_specs=[q_spec, kv...]
    reduce_sum x4 -> x2, other arithmetic: 193 us -> 11.7 us  [the longest x1 7.44 us: local_step(): d_gain = lax.psum(jnp.sum(d_normed * x_hat, axis=(0, 1)), 'sp')]
    all_to_all x0 -> x2, blocking collectives: none -> 142 us  [local_step(): o_all = lax.all_to_all(o_t, 'sp', 0, 0, tiled=True)]
    all_gather x0 -> x6, waiting for transfers between devices: none -> 134 us  [the longest x2 134 us: local_step(): lax.all_gather(normed[b], 'sp', axis=0, tiled=True)]
    all_to_all x13 -> x0, local copies, waits for them, and re-layouts: 99.9 us -> none  [the longest x2 19.2 us: local_step(): o_local = lax.all_to_all(o_heads, 'sp', 1, 2, tiled=True)]
    unnamed x76 -> x59, local copies, waits for them, and re-layouts: 100 us -> 22.3 us
  transfers between devices with their start and end apart: 9 -> 8, of which waited for: 7 -> 4; matrix products, arithmetic and copies ran while one was open for 9% -> 19% of each run, Pallas kernels for 0% -> 38%
where the time goes in v1:
time: 1170 us
  Pallas kernels  441 us (38%)
  waiting for transfers between devices  240 us (21%)
  matrix products  165 us (14%)
  blocking collectives  148 us (13%)
  local copies, waits for them, and re-layouts  109 us (9%)
  other arithmetic  36.6 us (3%)
  between operations  14.8 us (1%)
    pallas_call x2, Pallas kernels, attn_bwd(): pl.pallas_call(bwd_kernel, grid=(num_kv, seq // BQ), in_specs=[q_spec, kv...  277 us
    dot_general x12, matrix products, dot32(): return jnp.einsum(spec, lhs, rhs, preferred_element_type=jnp.float32)  165 us
    pallas_call x2, Pallas kernels, attn_fwd(): pl.pallas_call(fwd_kernel, grid=(num_kv, seq // BQ), in_specs=[pl.BlockSp...  164 us
    all_to_all x2, blocking collectives, local_step(): o_all = lax.all_to_all(o_t, 'sp', 0, 0, tiled=True)  142 us
    all_gather x2, waiting for transfers between devices, local_step(): lax.all_gather(normed[b], 'sp', axis=0, tiled=True)  134 us
    all_to_all x2, waiting for transfers between devices, local_step(): d_all = lax.all_to_all(d_qkv, 'sp', 0, 0, tiled=True)  106 us
    slice x2, local copies, waits for them, and re-layouts, local_step(): d_wq = d_wqkv[:, :, :q_feats].reshape(d_model, -1, HD)  28 us
  transfers between devices with their start and end apart: 8, of which 4 were waited for; matrix products, arithmetic and copies ran while one was open for 19% of the time, Pallas kernels for 38%

profile of v1, /device:TPU:0, one launch (start us, length us, event | category | flops | bytes accessed | tf_op | source)
XLA Modules:
  0.0 1165.8 jit_solution(8088653403293568987)
XLA Ops:
  7.2 4.2 fusion.11
  13.4 3.3 fusion.45
  17.5 6.7 fusion.44
  24.8 1.7 constant_dynamic-slice_fusion.2
  26.5 2.8 constant_dynamic-slice_fusion
  30.8 68.7 %all-gather.16.cloned.1.call-done = bf16[1,3072,2048]{2,1,0:T(8,128)(2,1)} async-done(((bf16[1,768,2048]{2,1,0:T(8,128)(2,1)}), bf16[1,3072,2048]{2,1,0:T(8,128)(2,1)}) %all-gather.16.cloned.1.call-update) | async-done | bytes 12582928 | tf_op jit(solution)/shard_map/all_gather | solution.py:275
  99.6 15.6 %fusion.17 = f32[768,3072]{1,0:T(8,128)} fusion(bf16[1,3072,2048]{2,1,0:T(8,128)(2,1)} %all-gather.16.cloned.1.call-done, bf16[2048,128]{0,1:T(8,128)(2,1)S(1)} %bitcast.112, bf16[2048,128]{0,1:T(8,128)(2,1)} %bitcast.114, bf16[2048,512]{0,1:T(8,128)(2,1)S(1)} %bitcast.110), kind=kOutput, calls=%fused_computation.22 | convolution fusion | flops 9673113600 | bytes 25165824 | tf_op jit(solution)/shard_map/df,td->ft/dot_general | solution.py:254
  116.8 64.9 %all-gather.14.cloned.1.call-done = bf16[1,3072,2048]{2,1,0:T(8,128)(2,1)} async-done(((bf16[1,768,2048]{2,1,0:T(8,128)(2,1)}), bf16[1,3072,2048]{2,1,0:T(8,128)(2,1)}) %all-gather.14.cloned.1.call-update) | async-done | bytes 12582928 | tf_op jit(solution)/shard_map/all_gather | solution.py:275
  181.7 15.7 %fusion.19 = f32[768,3072]{1,0:T(8,128)} fusion(bf16[1,3072,2048]{2,1,0:T(8,128)(2,1)} %all-gather.14.cloned.1.call-done, bf16[2048,128]{0,1:T(8,128)(2,1)S(1)} %bitcast.113, bf16[2048,128]{0,1:T(8,128)(2,1)S(1)} %bitcast.115, bf16[2048,512]{0,1:T(8,128)(2,1)} %bitcast.111), kind=kOutput, calls=%fused_computation.24 | convolution fusion | flops 9673113600 | bytes 25165824 | tf_op jit(solution)/shard_map/df,td->ft/dot_general | solution.py:254
  203.2 1.8 slice-done.1
  205.0 1.8 subtract_convert_fusion.1
  207.2 2.1 pad_maximum_fusion.10
  209.9 82.2 %attn_fwd.2 = (bf16[4,512,768]{2,1,0:T(8,128)(2,1)S(1)}, f32[2,8,3072]{2,1,0:T(8,128)S(1)}) custom-call(bf16[512,3072]{1,0:T(8,128)(2,1)S(1)} %bitcast.87, bf16[128,3072]{1,0:T(8,128)(2,1)S(1)} %bitcast.91, bf16[128,3072]{1,0:T(8,128)(2,1)S(1)} %slice.124.vt_ref), custom_call_target="tpu_custom_call" | custom-call | flops 38654705664 | bytes 9437184 | tf_op jit(solution)/shard_map/attn_fwd/pallas_call | solution.py:168
  293.7 12.0 %fusion.47 = f32[512,2048,1]{1,0,2:T(8,128)} fusion(bf16[4,512,768]{2,1,0:T(8,128)(2,1)} %copy-done, bf16[4,768,2048]{2,1,0:T(8,128)(2,1)} %bitcast.118), kind=kOutput, calls=%fused_computation.83 | convolution fusion | flops 6442450944 | bytes 19922944 | tf_op jit(solution)/shard_map/jft,jtd->fd/dot_general | solution.py:254
  305.7 82.0 %attn_fwd.3 = (bf16[4,512,768]{2,1,0:T(8,128)(2,1)S(1)}, f32[2,8,3072]{2,1,0:T(8,128)S(1)}) custom-call(bf16[512,3072]{1,0:T(8,128)(2,1)S(1)} %bitcast.90, bf16[128,3072]{1,0:T(8,128)(2,1)S(1)} %bitcast.93, bf16[128,3072]{1,0:T(8,128)(2,1)S(1)} %slice.123.vt_ref), custom_call_target="tpu_custom_call" | custom-call | flops 38654705664 | bytes 9437184 | tf_op jit(solution)/shard_map/attn_fwd/pallas_call | solution.py:168
  387.7 1.7 copy-done.2
  389.3 13.9 %bitcast_add_fusion.1 = f32[512,2048]{1,0:T(8,128)} fusion(f32[512,2048,1]{1,0,2:T(8,128)} %fusion.47, bf16[4,512,768]{2,1,0:T(8,128)(2,1)} %copy-done.2, bf16[4,768,2048]{2,1,0:T(8,128)(2,1)} %bitcast.119), kind=kOutput, calls=%fused_computation.34 | convolution fusion | flops 6443499520 | bytes 24117248 | tf_op jit(solution)/shard_map/jft,jtd->fd/dot_general | solution.py:254
  403.3 13.2 %fusion.26.dot_ref = bf16[512,3072]{1,0:T(8,128)(2,1)} fusion(bf16[1,3072,2048]{2,1,0:T(8,128)(2,1)} %all-gather.20.cloned.1.call-done, bf16[4,512,2048]{2,1,0:T(8,128)(2,1)} %bitcast.120, s32[]{:T(128)S(6)} %select_n.13), kind=kOutput, calls=%fused_computation.33 | convolution fusion | flops 6444023808 | bytes 17825796 | tf_op jit(solution)/shard_map/fd,td->ft/dot_general | solution.py:254
  416.5 138.5 %attn_bwd.3 = (bf16[4,512,768]{2,1,0:T(8,128)(2,1)}, bf16[4,128,768]{2,1,0:T(8,128)(2,1)S(1)}, bf16[4,128,768]{2,1,0:T(8,128)(2,1)S(1)}) custom-call(bf16[512,3072]{1,0:T(8,128)(2,1)} %bitcast.89, bf16[128,3072]{1,0:T(8,128)(2,1)S(1)} %bitcast.94, bf16[128,3072]{1,0:T(8,128)(2,1)S(1)} %slice.123.vt_ref, bf16[512,3072]{1,0:T(8,128)(2,1)} %fusion.26.dot_ref, ...), custom_call_target="tpu_custom_call" | custom-call | flops 96636764160 | bytes 15728640 | tf_op jit(solution)/shard_map/attn_bwd/pallas_call | solution.py:210
  555.0 2.1 constant_dynamic-update-slice_fusion.5
  557.2 14.7 %fusion.23.dot_ref = bf16[512,3072]{1,0:T(8,128)(2,1)} fusion(bf16[1,3072,2048]{2,1,0:T(8,128)(2,1)} %all-gather.18.cloned.1.call-done, bf16[4,512,2048]{2,1,0:T(8,128)(2,1)} %bitcast.121, s32[]{:T(128)S(6)} %select_n.13), kind=kOutput, calls=%fused_computation.32 | convolution fusion | flops 6444023808 | bytes 17825796 | tf_op jit(solution)/shard_map/fd,td->ft/dot_general | solution.py:254
  571.9 138.8 %attn_bwd.2 = (bf16[4,512,768]{2,1,0:T(8,128)(2,1)}, bf16[4,128,768]{2,1,0:T(8,128)(2,1)S(1)}, bf16[4,128,768]{2,1,0:T(8,128)(2,1)S(1)}) custom-call(bf16[512,3072]{1,0:T(8,128)(2,1)} %bitcast.88, bf16[128,3072]{1,0:T(8,128)(2,1)S(1)} %bitcast.92, bf16[128,3072]{1,0:T(8,128)(2,1)S(1)} %copy-done.7, bf16[512,3072]{1,0:T(8,128)(2,1)} %fusion.23.dot_ref, ...), custom_call_target="tpu_custom_call" | custom-call | flops 96636764160 | bytes 15728640 | tf_op jit(solution)/shard_map/attn_bwd/pallas_call | solution.py:210
  710.7 2.1 constant_dynamic-update-slice_fusion.2
  712.9 14.8 %fusion.46 = f32[2048,768,1]{1,0,2:T(8,128)S(1)} fusion(bf16[4,768,2048]{2,1,0:T(8,128)(2,1)} %bitcast.117, bf16[4,768,768]{2,1,0:T(8,128)(2,1)S(1)} %constant_dynamic-update-slice_fusion), kind=kOutput, calls=%fused_computation.82 | convolution fusion | flops 9663676416 | bytes 23592960 | tf_op jit(solution)/shard_map/jtd,jft->df/dot_general | solution.py:254
  727.7 15.3 %bitcast_add_fusion = f32[2048,768]{1,0:T(8,128)} fusion(f32[2048,768,1]{1,0,2:T(8,128)S(1)} %fusion.46, bf16[4,768,2048]{2,1,0:T(8,128)(2,1)} %bitcast.116, bf16[4,768,768]{2,1,0:T(8,128)(2,1)S(1)} %constant_dynamic-update-slice_fusion.3), kind=kOutput, calls=%fused_computation.27 | convolution fusion | flops 9665249280 | bytes 29884416 | tf_op jit(solution)/shard_map/jtd,jft->df/dot_general | solution.py:254
  743.0 1.9 copy-done.3
  744.9 67.3 %all_to_all.20 = bf16[4,512,768]{2,1,0:T(8,128)(2,1)} all-to-all(bf16[4,512,768]{2,1,0:T(8,128)(2,1)S(1)} %copy-done.3), channel_id=1, replica_groups=mesh['dp'=2,'sp'=4] {'sp'}, dimensions={0} | all-to-all | bytes 6291456 | tf_op jit(solution)/shard_map/all_to_all | solution.py:293
  812.2 74.3 %all_to_all.21 = bf16[4,512,768]{2,1,0:T(8,128)(2,1)} all-to-all(bf16[4,512,768]{2,1,0:T(8,128)(2,1)S(1)} %copy-done.1), channel_id=1, replica_groups=mesh['dp'=2,'sp'=4] {'sp'}, dimensions={0} | all-to-all | bytes 6291456 | tf_op jit(solution)/shard_map/all_to_all | solution.py:293
  886.4 5.1 all-to-all-start.3
  891.5 2.5 copy.27
  894.0 4.0 copy.26
  898.0 11.4 copy.25
  909.4 86.6 %all-to-all-done.3 = bf16[4,768,768]{2,1,0:T(8,128)(2,1)} async-done(((bf16[4,768,768]{2,1,0:T(8,128)(2,1)}), bf16[4,768,768]{2,1,0:T(8,128)(2,1)}, u32[]{:S(2)}, u32[]{:S(2)}) %all-to-all-start.3) | async-done | bytes 4718624 | tf_op jit(solution)/shard_map/all_to_all | solution.py:311
  996.0 5.1 all-to-all-start.2
  1001.1 11.0 convolution_bitcast_fusion
  1012.1 11.3 convolution_bitcast_fusion.1
  1023.4 12.6 %fusion.30 = bf16[1,768,2048]{2,1,0:T(8,128)(2,1)S(1)} fusion(bf16[4,768,768]{2,1,0:T(8,128)(2,1)} %all-to-all-done.3, bf16[2048,4,128]{2,0,1:T(8,128)(2,1)S(1)} %copy-done.18, bf16[2048,4,128]{2,0,1:T(8,128)(2,1)S(1)} %copy-done.19, bf16[2048,4,512]{2,0,1:T(8,128)(2,1)S(1)} %bitcast.105), kind=kOutput, calls=%fused_computation.45 | convolution fusion | flops 9702998016 | bytes 20447232 | tf_op jit(solution)/shard_map/jft,djf->td/dot_general | solution.py:254
  1036.0 18.9 %all-to-all-done.2 = bf16[4,768,768]{2,1,0:T(8,128)(2,1)} async-done(((bf16[4,768,768]{2,1,0:T(8,128)(2,1)}), bf16[4,768,768]{2,1,0:T(8,128)(2,1)}, u32[]{:S(2)}, u32[]{:S(2)}) %all-to-all-start.2) | async-done | bytes 4718624 | tf_op jit(solution)/shard_map/all_to_all | solution.py:311
  1054.9 14.6 %fusion.29 = bf16[1,768,2048]{2,1,0:T(8,128)(2,1)S(1)} fusion(bf16[4,768,768]{2,1,0:T(8,128)(2,1)} %all-to-all-done.2, bf16[2048,4,128]{2,0,1:T(8,128)(2,1)} %copy.27, bf16[2048,4,128]{2,0,1:T(8,128)(2,1)} %copy.26, bf16[2048,4,512]{2,0,1:T(8,128)(2,1)} %copy.25), kind=kOutput, calls=%fused_computation.44 | convolution fusion | flops 9702998016 | bytes 20447232 | tf_op jit(solution)/shard_map/jft,djf->td/dot_general | solution.py:254
  1069.6 7.4 fusion.10
  1077.0 6.5 psum.7
  1083.5 17.1 %fusion.7 = (bf16[2,768,2048]{2,1,0:T(8,128)(2,1)}, bf16[2,768,2048]{2,1,0:T(8,128)(2,1)}) fusion(bf16[2,768,2048]{2,1,0:T(8,128)(2,1)} %param.7, bf16[2,768,2048]{2,1,0:T(8,128)(2,1)} %param.8, f32[2,768]{1,0:T(2,128)S(1)} %broadcast_multiply_fusion, f32[2048]{0:T(1024)S(1)} %copy-done.24, f32[2,768]{1,0:T(2,128)S(1)} %copy-done.22, ...), kind=kLoop, calls=%fused_computation.11 | loop fusion | flops 44040192 | bytes 44060672 | tf_op jit(solution)/shard_map/convert_element_type | solution.py:325
  1100.7 7.5 fusion.43
  1108.2 11.7 %slice.102 = f32[2048,4,512]{2,0,1:T(8,128)} slice(f32[2048,4,768]{2,0,1:T(8,128)} %bitcast.96), slice={[0:2048], [0:4], [0:512]} | slice | bytes 33554432 | tf_op jit(solution)/shard_map/slice | solution.py:317
  1119.9 16.3 %copy.32 = f32[2048,4,512]{0,2,1:T(8,128)} copy(f32[2048,4,512]{2,0,1:T(8,128)} %slice.102) | data formatting | bytes 33554432 | tf_op jit(solution)/shard_map/slice | solution.py:317
  1136.2 5.3 copy.34
  1141.6 5.3 copy.33
  1146.9 11.8 %copy.46 = f32[32,64,2048]{2,1,0:T(8,128)} copy(f32[32,64,2048]{2,1,0:T(8,128)} %bitcast.101) | data formatting | bytes 33554432
  (91 shorter events, 14.9 us)
Async XLA Ops:
  7.2 4.3 copy-start.23
  7.2 92.4 %all-gather.16.cloned.1.call-start = ((), (), s32[]{:S(2)}) async-start(), calls=%async_computation.6 | async-start | bytes 15728640 | tf_op jit(solution)/shard_map/all_gather | solution.py:275
  7.2 4.6 copy-start.10
  11.8 1.5 copy-start.21
  16.7 165.0 %all-gather.14.cloned.1.call-start = ((), (), s32[]{:S(2)}) async-start(), calls=%async_computation.5 | async-start | bytes 15728640 | tf_op jit(solution)/shard_map/all_gather | solution.py:275
  17.4 276.3 %all-gather.18.cloned.1.call-start = ((), (), s32[]{:S(2)}) async-start(), calls=%async_computation.7 | async-start | bytes 15728640 | tf_op jit(solution)/shard_map/all_gather | solution.py:276
  24.1 365.2 %all-gather.20.cloned.1.call-start = ((), (), s32[]{:S(2)}) async-start(), calls=%async_computation.8 | async-start | bytes 15728640 | tf_op jit(solution)/shard_map/all_gather | solution.py:276
  24.7 1075.9 %all-gather.12.cloned.1.call-start = ((), (), s32[]{:S(2)}) async-start(), calls=%async_computation.4 | async-start | bytes 20971520 | tf_op jit(solution)/shard_map/all_gather | solution.py:305
  26.5 73.1 %copy-start.17 = (bf16[2048,8,64]{0,2,1:T(8,128)(2,1)}, bf16[2048,8,64]{0,2,1:T(8,128)(2,1)S(1)}, u32[]{:S(2)}) copy-start(bf16[2048,8,64]{0,2,1:T(8,128)(2,1)S(1)} %constant_dynamic-slice_fusion.2) | copy-start | bytes 6291460
  116.8 64.9 %copy-start.20 = (bf16[2048,2,64]{0,2,1:T(8,128)(2,1)S(1)}, bf16[2048,2,64]{0,2,1:T(8,128)(2,1)}, u32[]{:S(2)}) copy-start(bf16[2048,2,64]{0,2,1:T(8,128)(2,1)} %get-tuple-element.52) | copy-start | bytes 1572868
  198.9 10.4 copy-start.6
  198.9 1.7 slice-start
  199.0 2.2 slice-start.2
  199.0 4.3 slice-start.3
  199.0 6.1 slice-start.1
  201.6 7.7 copy-start.8
  207.2 2.7 copy-start.4
  292.0 1.7 copy-start
  293.7 12.0 %copy-start.5 = (bf16[8,2,32,3072]{3,2,1,0:T(8,128)(2,1)S(1)}, bf16[8,2,32,3072]{3,2,1,0:T(8,128)(2,1)}, u32[]{:S(2)}) copy-start(bf16[8,2,32,3072]{3,2,1,0:T(8,128)(2,1)} %pad_maximum_fusion.10) | copy-start | bytes 9437188
  387.7 1.7 copy-start.2
  403.2 697.4 %all-gather.22.cloned.1.call-start = ((), (), s32[]{:S(2)}) async-start(), calls=%async_computation.9 | async-start | bytes 31457280 | tf_op jit(solution)/shard_map/all_gather | solution.py:315
  557.2 170.5 %copy-start.11 = (bf16[4,768,768]{2,1,0:T(8,128)(2,1)}, bf16[4,768,768]{2,1,0:T(8,128)(2,1)S(1)}, u32[]{:S(2)}) copy-start(bf16[4,768,768]{2,1,0:T(8,128)(2,1)S(1)} %constant_dynamic-update-slice_fusion.3) | copy-start | bytes 14155780
  557.2 14.7 %copy-start.7 = (bf16[128,3072]{1,0:T(8,128)(2,1)S(1)}, bf16[128,3072]{1,0:T(8,128)(2,1)}, u32[]{:S(2)}) copy-start(bf16[128,3072]{1,0:T(8,128)(2,1)} %copy-done.6) | copy-start | bytes 2359300
  557.2 14.7 %copy-start.9 = (bf16[2,2,32,3072]{3,2,1,0:T(8,128)(2,1)S(1)}, bf16[2,2,32,3072]{3,2,1,0:T(8,128)(2,1)}, u32[]{:S(2)}) copy-start(bf16[2,2,32,3072]{3,2,1,0:T(8,128)(2,1)} %copy-done.8) | copy-start | bytes 2359300
  712.9 14.8 %copy-start.12 = (bf16[4,768,768]{2,1,0:T(8,128)(2,1)}, bf16[4,768,768]{2,1,0:T(8,128)(2,1)S(1)}, u32[]{:S(2)}) copy-start(bf16[4,768,768]{2,1,0:T(8,128)(2,1)S(1)} %constant_dynamic-update-slice_fusion) | copy-start | bytes 14155780
  743.0 1.9 copy-start.3
  744.9 67.3 %copy-start.1 = (bf16[4,512,768]{2,1,0:T(8,128)(2,1)S(1)}, bf16[4,512,768]{2,1,0:T(8,128)(2,1)}, u32[]{:S(2)}) copy-start(bf16[4,512,768]{2,1,0:T(8,128)(2,1)} %copy-done) | copy-start | bytes 9437188
  886.4 5.1 copy-start.14
  886.4 109.5 %all-to-all-start.3 = ((bf16[4,768,768]{2,1,0:T(8,128)(2,1)}), bf16[4,768,768]{2,1,0:T(8,128)(2,1)}, u32[]{:S(2)}, u32[]{:S(2)}) async-start(bf16[4,768,768]{2,1,0:T(8,128)(2,1)} %copy-done.11), calls=%async_computation.3 | async-start | bytes 9437184 | tf_op jit(solution)/shard_map/all_to_all | solution.py:311
  909.4 91.7 %copy-start.15 = (bf16[4,512,768]{2,1,0:T(8,128)(2,1)S(1)}, bf16[4,512,768]{2,1,0:T(8,128)(2,1)}, u32[]{:S(2)}) copy-start(bf16[4,512,768]{2,1,0:T(8,128)(2,1)} %all_to_all.20) | copy-start | bytes 9437188
  996.0 59.0 %all-to-all-start.2 = ((bf16[4,768,768]{2,1,0:T(8,128)(2,1)}), bf16[4,768,768]{2,1,0:T(8,128)(2,1)}, u32[]{:S(2)}, u32[]{:S(2)}) async-start(bf16[4,768,768]{2,1,0:T(8,128)(2,1)} %copy-done.12), calls=%async_computation.2 | async-start | bytes 9437184 | tf_op jit(solution)/shard_map/all_to_all | solution.py:311
  1001.1 11.0 copy-start.16
  1001.1 22.3 %slice-start.4 = ((s8[8388608]{0:T(1024)(128)(4,1)}), s8[4194304]{0:T(1024)(128)(4,1)S(1)}, s32[]{:S(2)}) async-start(s8[8388608]{0:T(1024)(128)(4,1)} %bitcast.104), calls=%async_computation.14 | async-start | bytes 8388608
  1012.1 11.3 slice-start.5
  1012.1 11.3 copy-start.18
  1012.1 11.3 copy-start.19
  1036.0 33.6 %copy-start.22 = (f32[2,768]{1,0:T(2,128)S(1)}, f32[2,768]{1,0:T(2,128)}, u32[]{:S(2)}) copy-start(f32[2,768]{1,0:T(2,128)} %copy-done.21) | copy-start | bytes 18436
  1036.0 33.6 %copy-start.24 = (f32[2048]{0:T(1024)S(1)}, f32[2048]{0:T(1024)}, u32[]{:S(2)}) copy-start(f32[2048]{0:T(1024)} %param.9) | copy-start | bytes 24580
  1069.6 7.5 copy-start.13
Sparse Core Ops, SparseCore 0:
  16.8 82.7 all-gather.15
  101.7 79.9 all-gather.13
  183.8 79.9 all-gather.17
  265.7 79.9 all-gather.19
  403.4 104.1 all-gather.11
  743.1 263.9 all-gather.21
